TPU v7x, 32 devices: a whole 2x2x4 slice. The times are simulated.
32 devices in a mesh: cand: 4 (over x, core), tp: 8 (over z, y).
Axes of the slice: x: 2, y: 2, z: 4, core: 2. Of those that a mesh axis runs over, the one named last changes fastest.
Arguments:
- start_state: float32 [128], replicated, may hold values from -6 to 6
- goal: float32 [128], replicated, may hold values from -6 to 6
- mean_prev: float32 [128], replicated, may hold values from -0.5 to 0.5
- std_prev: float32 [128], replicated, may hold values from 0.1 to 0.5
- noise: float32 [768, 128], P('cand'), may hold values from -23 to 23
- members: int32 [768, 1], P('cand'), may hold values from 0 to 3; in each aligned block of 192 rows (0 to 191, 192 to 383, ...) at most 60 rows name the same one
- elites: int32 [96], replicated, may hold values from 0 to 767, as said below
- w_in: bfloat16 [4, 144, 4096], P(None, None, 'tp'), may hold values from -0.5 to 0.5
- w_hid: bfloat16 [4, 4096, 4096], P(None, None, 'tp'), may hold values from -0.09375 to 0.09375
- w_out: bfloat16 [4, 4096, 128], P(None, 'tp'), may hold values from -0.09375 to 0.09375
Outputs:
- scores: float32 [768], P('cand')
- new_mean: float32 [128], replicated
- new_std: float32 [128], replicated
Inputs may be any that keep to these rules, and one draw needn't show every extreme that they name: `members`: among the candidates of one index of cand no member is named more than 60 times. `elites`: 96 distinct candidate numbers.
All inputs are finite; a program needn't handle non-finite values.
Results may differ from a plain program's by a relative error of at most 0.0085.
Values may be sent and summed in bfloat16 or wider, within the bound.
A program may use at most 64 MiB of HBM per device.

v0:
```python
import jax
import jax.numpy as jnp
from jax import lax
from jax.sharding import PartitionSpec as P

HORIZON = 8


def reward_of(states, goal, action):
    return -jnp.mean((states - goal) ** 2, axis=-1) - 0.1 * jnp.mean(action * action, axis=-1)


def on_device(start_state, goal, mean_prev, std_prev, noise, members, elites, w_in, w_hid, w_out):
    local_count = noise.shape[0]
    member_count = w_in.shape[0]
    state_width = start_state.shape[0]
    capacity = 5 * local_count // 16
    action_width = mean_prev.shape[0] // HORIZON
    actions = mean_prev[None, :] + std_prev[None, :] * noise
    onehot = (members == jnp.arange(member_count, dtype=jnp.int32)[None, :]).astype(jnp.float32)
    before = jnp.cumsum(onehot, axis=0) - onehot
    position = jnp.sum(before * onehot, axis=1).astype(jnp.int32)
    slot_number = members[:, 0] * capacity + position
    dispatch = (
        slot_number[None, :] == jnp.arange(member_count * capacity, dtype=jnp.int32)[:, None]
    ).astype(jnp.float32)
    slot_actions = jnp.dot(dispatch, actions, precision=lax.Precision.HIGHEST)
    slot_actions = slot_actions.reshape(member_count, capacity, HORIZON, action_width)
    input_layer = lax.all_gather(w_in, "tp", axis=2, tiled=True)

    def rollout(first, count):
        layer_in = input_layer[first : first + count]
        hid_rows = w_hid[first : first + count]
        out_rows = w_out[first : first + count]
        states = jnp.zeros((count, capacity, state_width), jnp.float32) + start_state[None, None, :]
        running = jnp.zeros((count, capacity), jnp.float32)
        for step_index in range(HORIZON):
            action = slot_actions[first : first + count, :, step_index, :]
            inputs = jnp.concatenate([states, action], axis=2).astype(jnp.bfloat16)
            first_pre = jnp.einsum(
                "mck,mkh->mch", inputs, layer_in, preferred_element_type=jnp.float32
            )
            hidden_one = jax.nn.silu(first_pre).astype(jnp.bfloat16)
            second_pre = jnp.einsum(
                "mck,mkh->mch", hidden_one, hid_rows, preferred_element_type=jnp.float32
            )
            hidden_two = jax.nn.silu(second_pre).astype(jnp.bfloat16)
            partial_change = jnp.einsum(
                "mck,mks->mcs", hidden_two, out_rows, preferred_element_type=jnp.float32
            )
            change = lax.psum(partial_change, "tp")
            states = states + change
            running = running + reward_of(states, goal[None, None, :], action)
        return running

    slot_returns = jnp.concatenate([rollout(member, 1) for member in range(member_count)], axis=0)
    returns = jnp.dot(
        slot_returns.reshape(member_count * capacity), dispatch, precision=lax.Precision.HIGHEST
    )
    first_index = lax.axis_index("cand") * local_count
    numbers = first_index + jnp.arange(local_count, dtype=jnp.int32)
    chosen = jnp.sum((elites[:, None] == numbers[None, :]).astype(jnp.float32), axis=0)
    count_all = local_count * lax.axis_size("cand")
    return_sum = lax.psum(jnp.sum(returns), "cand")
    return_mean = return_sum / count_all
    return_spread = lax.psum(jnp.sum((returns - return_mean) ** 2), "cand")
    return_var = return_spread / count_all
    scores = (returns - return_mean) / jnp.sqrt(return_var + 1e-06)
    weights = chosen * (0.5 + jax.nn.sigmoid(scores))
    weight_sum, first_moment = lax.psum(
        (jnp.sum(weights), jnp.dot(weights, actions, precision=lax.Precision.HIGHEST)), "cand"
    )
    new_mean = first_moment / weight_sum
    action_spread = lax.psum(
        jnp.dot(weights, (actions - new_mean[None, :]) ** 2, precision=lax.Precision.HIGHEST),
        "cand",
    )
    new_var = action_spread / weight_sum
    new_std = jnp.sqrt(new_var + 1e-06)
    return (scores, new_mean, new_std)


def solution(mesh):
    placed = (
        P(),
        P(),
        P(),
        P(),
        P("cand", None),
        P("cand", None),
        P(),
        P(None, None, "tp"),
        P(None, None, "tp"),
        P(None, "tp", None),
    )
    return jax.shard_map(
        on_device, mesh=mesh, in_specs=placed, out_specs=(P("cand"), P(), P()), check_vma=False
    )
```

profile of v0, /device:TPU:0, one launch (start us, length us, event | category | flops | bytes accessed | tf_op | source)
XLA Modules:
  0.0 847.4 jit_solution(5525363201203804489)
XLA Ops:
  8.7 1.2 reduce-window.6
  11.7 1.2 fusion.129
  16.0 77.4 %all-gather.2.cloned.1.call-done = bf16[4,144,4096]{2,1,0:T(8,128)(2,1)} async-done(((bf16[4,144,512]{2,1,0:T(8,128)(2,1)}), bf16[4,144,4096]{2,1,0:T(8,128)(2,1)}) %all-gather.2.cloned.1.call-update) | async-done | bytes 4718608 | tf_op jit(solution)/shard_map/all_gather | solution.py:29
  93.4 3.7 multiply_convert_fusion.109
  97.1 0.8 convolution_bitcast_fusion.15
  97.9 3.7 multiply_convert_fusion.133
  102.3 3.7 multiply_convert_fusion.157
  106.0 0.8 convolution_bitcast_fusion.31
  106.8 3.7 multiply_convert_fusion.85
  111.8 69.2 %all-reduce.33.cloned.1.call-done = (f32[1,60,128]{2,1,0:T(8,128)}, f32[1,60,128]{2,1,0:T(8,128)}, f32[1,60,128]{2,1,0:T(8,128)}, f32[1,60,128]{2,1,0:T(8,128)}) async-done(((f32[1,60,128]{2,1,0:T(8,128)}, f32[1,60,128]{2,1,0:T(8,128)}, f32[1,60,128]{2,1,0:T(8,128)}, f32[1,60,128]{2,1,0:T(8,128)}), (f32[1,60,128]{2,1,0:T(8,128)}, f32[1,60,128]{2,1,0:T(8,128)}, f32[1,60,128]{2,1,0:T(8,128)}, ...) | async-done | bytes 122896 | tf_op jit(solution)/shard_map/psum | solution.py:51
  180.9 0.8 fusion.485
  181.7 3.7 multiply_convert_fusion.154
  186.2 3.7 multiply_convert_fusion.82
  190.7 3.7 multiply_convert_fusion.106
  195.1 3.7 multiply_convert_fusion.130
  200.4 69.7 %all-reduce.31.cloned.1.call-done = (f32[1,60,128]{2,1,0:T(8,128)}, f32[1,60,128]{2,1,0:T(8,128)}, f32[1,60,128]{2,1,0:T(8,128)}, f32[1,60,128]{2,1,0:T(8,128)}) async-done(((f32[1,60,128]{2,1,0:T(8,128)}, f32[1,60,128]{2,1,0:T(8,128)}, f32[1,60,128]{2,1,0:T(8,128)}, f32[1,60,128]{2,1,0:T(8,128)}), (f32[1,60,128]{2,1,0:T(8,128)}, f32[1,60,128]{2,1,0:T(8,128)}, f32[1,60,128]{2,1,0:T(8,128)}, ...) | async-done | bytes 122896 | tf_op jit(solution)/shard_map/psum | solution.py:51
  270.1 0.8 convert_bitcast_fusion.50
  271.0 3.7 multiply_convert_fusion.151
  274.7 0.8 convolution_bitcast_fusion.29
  275.5 3.7 multiply_convert_fusion.79
  279.9 3.7 multiply_convert_fusion.103
  283.6 0.8 convolution_bitcast_fusion.13
  284.4 3.7 multiply_convert_fusion.127
  289.5 69.9 %all-reduce.29.cloned.1.call-done = (f32[1,60,128]{2,1,0:T(8,128)}, f32[1,60,128]{2,1,0:T(8,128)}, f32[1,60,128]{2,1,0:T(8,128)}, f32[1,60,128]{2,1,0:T(8,128)}) async-done(((f32[1,60,128]{2,1,0:T(8,128)}, f32[1,60,128]{2,1,0:T(8,128)}, f32[1,60,128]{2,1,0:T(8,128)}, f32[1,60,128]{2,1,0:T(8,128)}), (f32[1,60,128]{2,1,0:T(8,128)}, f32[1,60,128]{2,1,0:T(8,128)}, f32[1,60,128]{2,1,0:T(8,128)}, ...) | async-done | bytes 122896 | tf_op jit(solution)/shard_map/psum | solution.py:51
  359.4 0.8 convert_bitcast_fusion.35
  360.2 3.7 multiply_convert_fusion.148
  364.7 3.7 multiply_convert_fusion.76
  368.4 0.8 convolution_bitcast_fusion.4
  369.2 3.7 multiply_convert_fusion.100
  373.6 3.7 multiply_convert_fusion.124
  377.3 0.8 convolution_bitcast_fusion.20
  378.8 69.9 %all-reduce.27.cloned.1.call-done = (f32[1,60,128]{2,1,0:T(8,128)}, f32[1,60,128]{2,1,0:T(8,128)}, f32[1,60,128]{2,1,0:T(8,128)}, f32[1,60,128]{2,1,0:T(8,128)}) async-done(((f32[1,60,128]{2,1,0:T(8,128)}, f32[1,60,128]{2,1,0:T(8,128)}, f32[1,60,128]{2,1,0:T(8,128)}, f32[1,60,128]{2,1,0:T(8,128)}), (f32[1,60,128]{2,1,0:T(8,128)}, f32[1,60,128]{2,1,0:T(8,128)}, f32[1,60,128]{2,1,0:T(8,128)}, ...) | async-done | bytes 122896 | tf_op jit(solution)/shard_map/psum | solution.py:51
  449.4 3.7 multiply_convert_fusion.145
  453.9 3.7 multiply_convert_fusion.73
  457.6 0.8 convolution_bitcast_fusion.3
  458.4 3.7 multiply_convert_fusion.97
  462.1 0.8 convolution_bitcast_fusion.11
  462.9 3.7 multiply_convert_fusion.121
  466.6 0.8 convolution_bitcast_fusion.19
  468.3 69.7 %all-reduce.25.cloned.1.call-done = (f32[1,60,128]{2,1,0:T(8,128)}, f32[1,60,128]{2,1,0:T(8,128)}, f32[1,60,128]{2,1,0:T(8,128)}, f32[1,60,128]{2,1,0:T(8,128)}) async-done(((f32[1,60,128]{2,1,0:T(8,128)}, f32[1,60,128]{2,1,0:T(8,128)}, f32[1,60,128]{2,1,0:T(8,128)}, f32[1,60,128]{2,1,0:T(8,128)}), (f32[1,60,128]{2,1,0:T(8,128)}, f32[1,60,128]{2,1,0:T(8,128)}, f32[1,60,128]{2,1,0:T(8,128)}, ...) | async-done | bytes 122896 | tf_op jit(solution)/shard_map/psum | solution.py:51
  538.7 3.7 multiply_convert_fusion.142
  543.2 3.7 multiply_convert_fusion.70
  547.7 3.7 multiply_convert_fusion.94
  552.2 3.7 multiply_convert_fusion.118
  557.2 70.0 %all-reduce.23.cloned.1.call-done = (f32[1,60,128]{2,1,0:T(8,128)}, f32[1,60,128]{2,1,0:T(8,128)}, f32[1,60,128]{2,1,0:T(8,128)}, f32[1,60,128]{2,1,0:T(8,128)}) async-done(((f32[1,60,128]{2,1,0:T(8,128)}, f32[1,60,128]{2,1,0:T(8,128)}, f32[1,60,128]{2,1,0:T(8,128)}, f32[1,60,128]{2,1,0:T(8,128)}), (f32[1,60,128]{2,1,0:T(8,128)}, f32[1,60,128]{2,1,0:T(8,128)}, f32[1,60,128]{2,1,0:T(8,128)}, ...) | async-done | bytes 122896 | tf_op jit(solution)/shard_map/psum | solution.py:51
  628.0 3.7 multiply_convert_fusion.139
  632.5 3.7 multiply_convert_fusion.67
  637.0 3.7 multiply_convert_fusion.91
  641.4 3.7 multiply_convert_fusion.115
  646.1 70.3 %all-reduce.21.cloned.1.call-done = (f32[1,60,128]{2,1,0:T(8,128)}, f32[1,60,128]{2,1,0:T(8,128)}, f32[1,60,128]{2,1,0:T(8,128)}, f32[1,60,128]{2,1,0:T(8,128)}) async-done(((f32[1,60,128]{2,1,0:T(8,128)}, f32[1,60,128]{2,1,0:T(8,128)}, f32[1,60,128]{2,1,0:T(8,128)}, f32[1,60,128]{2,1,0:T(8,128)}), (f32[1,60,128]{2,1,0:T(8,128)}, f32[1,60,128]{2,1,0:T(8,128)}, f32[1,60,128]{2,1,0:T(8,128)}, ...) | async-done | bytes 122896 | tf_op jit(solution)/shard_map/psum | solution.py:51
  717.2 3.7 multiply_convert_fusion.136
  721.7 3.7 multiply_convert_fusion.64
  726.2 3.7 multiply_convert_fusion.88
  729.9 0.8 convolution_bitcast_fusion.8
  730.7 3.7 multiply_convert_fusion.112
  735.2 70.5 %all-reduce.19.cloned.1.call-done = (f32[1,60,128]{2,1,0:T(8,128)}, f32[1,60,128]{2,1,0:T(8,128)}, f32[1,60,128]{2,1,0:T(8,128)}, f32[1,60,128]{2,1,0:T(8,128)}) async-done(((f32[1,60,128]{2,1,0:T(8,128)}, f32[1,60,128]{2,1,0:T(8,128)}, f32[1,60,128]{2,1,0:T(8,128)}, f32[1,60,128]{2,1,0:T(8,128)}), (f32[1,60,128]{2,1,0:T(8,128)}, f32[1,60,128]{2,1,0:T(8,128)}, f32[1,60,128]{2,1,0:T(8,128)}, ...) | async-done | bytes 122896 | tf_op jit(solution)/shard_map/psum | solution.py:51
  805.8 1.2 multiply_reduce_fusion.59
  807.0 1.2 multiply_reduce_fusion.33
  809.2 6.3 psum.291
  816.8 7.2 psum.292
  824.8 1.2 fusion.595
  826.1 6.6 all-reduce.9
  833.6 6.0 psum.295
  839.7 1.2 add_sqrt_fusion
  (193 shorter events, 33.2 us)
Async XLA Ops:
  7.2 86.2 %all-gather.2.cloned.1.call-start = ((), (), s32[]{:S(2)}) async-start(), calls=%async_computation | async-start | bytes 5308416 | tf_op jit(solution)/shard_map/all_gather | solution.py:29
  7.9 173.0 %all-reduce.33.cloned.1.call-start = ((), (), s32[]{:S(2)}) async-start(), calls=%async_computation.8 | async-start | bytes 262144 | tf_op jit(solution)/shard_map/psum | solution.py:51
  93.4 3.7 copy-start
  106.8 74.1 %copy-start.22 = (f32[128]{0:T(128)S(1)}, f32[128]{0:T(128)}, u32[]{:S(2)}) copy-start(f32[128]{0:T(128)} %param.10) | copy-start | bytes 1540
  111.3 158.8 %all-reduce.31.cloned.1.call-start = ((), (), s32[]{:S(2)}) async-start(), calls=%async_computation.7 | async-start | bytes 262144 | tf_op jit(solution)/shard_map/psum | solution.py:51
  195.1 75.0 %copy-start.2 = (f32[1,60,128]{2,1,0:T(8,128)S(1)}, f32[1,60,128]{2,1,0:T(8,128)}, u32[]{:S(2)}) copy-start(f32[1,60,128]{2,1,0:T(8,128)} %get-tuple-element.73) | copy-start | bytes 92164
  195.1 75.0 %copy-start.3 = (f32[1,60,128]{2,1,0:T(8,128)S(1)}, f32[1,60,128]{2,1,0:T(8,128)}, u32[]{:S(2)}) copy-start(f32[1,60,128]{2,1,0:T(8,128)} %get-tuple-element.74) | copy-start | bytes 92164
  195.1 75.0 %copy-start.4 = (f32[1,60,128]{2,1,0:T(8,128)S(1)}, f32[1,60,128]{2,1,0:T(8,128)}, u32[]{:S(2)}) copy-start(f32[1,60,128]{2,1,0:T(8,128)} %get-tuple-element.75) | copy-start | bytes 92164
  195.1 75.0 %copy-start.5 = (f32[1,60,128]{2,1,0:T(8,128)S(1)}, f32[1,60,128]{2,1,0:T(8,128)}, u32[]{:S(2)}) copy-start(f32[1,60,128]{2,1,0:T(8,128)} %get-tuple-element.76) | copy-start | bytes 92164
  199.6 159.8 %all-reduce.29.cloned.1.call-start = ((), (), s32[]{:S(2)}) async-start(), calls=%async_computation.6 | async-start | bytes 262144 | tf_op jit(solution)/shard_map/psum | solution.py:51
  288.9 159.8 %all-reduce.27.cloned.1.call-start = ((), (), s32[]{:S(2)}) async-start(), calls=%async_computation.5 | async-start | bytes 262144 | tf_op jit(solution)/shard_map/psum | solution.py:51
  360.2 4.5 copy-start.12
  360.2 4.5 copy-start.13
  378.1 159.8 %all-reduce.25.cloned.1.call-start = ((), (), s32[]{:S(2)}) async-start(), calls=%async_computation.4 | async-start | bytes 262144 | tf_op jit(solution)/shard_map/psum | solution.py:51
  449.4 4.5 copy-start.17
  453.9 4.5 copy-start.11
  458.4 4.5 copy-start.8
  467.4 159.8 %all-reduce.23.cloned.1.call-start = ((), (), s32[]{:S(2)}) async-start(), calls=%async_computation.3 | async-start | bytes 262144 | tf_op jit(solution)/shard_map/psum | solution.py:51
  538.7 4.5 copy-start.15
  543.2 4.5 copy-start.9
  547.7 4.5 copy-start.6
  556.7 159.7 %all-reduce.21.cloned.1.call-start = ((), (), s32[]{:S(2)}) async-start(), calls=%async_computation.2 | async-start | bytes 262144 | tf_op jit(solution)/shard_map/psum | solution.py:51
  628.0 4.5 copy-start.16
  632.5 4.5 copy-start.10
  637.0 4.5 copy-start.7
  645.9 159.8 %all-reduce.19.cloned.1.call-start = ((), (), s32[]{:S(2)}) async-start(), calls=%async_computation.1 | async-start | bytes 262144 | tf_op jit(solution)/shard_map/psum | solution.py:51
  717.2 4.5 copy-start.19
  721.7 4.5 copy-start.18
  726.2 4.5 copy-start.14
  730.7 75.1 %copy-start.23 = (f32[128]{0:T(128)S(1)}, f32[128]{0:T(128)}, u32[]{:S(2)}) copy-start(f32[128]{0:T(128)} %param.11) | copy-start | bytes 1540
  730.7 86.1 %copy-start.25 = (s32[96]{0:T(128)S(1)}, s32[96]{0:T(128)}, u32[]{:S(2)}) copy-start(s32[96]{0:T(128)} %param.16) | copy-start | bytes 1156
  730.7 95.3 %copy-start.1 = (f32[192,128]{1,0:T(8,128)S(1)}, f32[192,128]{1,0:T(8,128)}, u32[]{:S(2)}) copy-start(f32[192,128]{1,0:T(8,128)} %param.14) | copy-start | bytes 294916
  730.7 95.2 %copy-start.20 = (f32[128]{0:T(128)S(1)}, f32[128]{0:T(128)}, u32[]{:S(2)}) copy-start(f32[128]{0:T(128)} %param.13) | copy-start | bytes 1540
  730.7 95.2 %copy-start.21 = (f32[128]{0:T(128)S(1)}, f32[128]{0:T(128)}, u32[]{:S(2)}) copy-start(f32[128]{0:T(128)} %param.12) | copy-start | bytes 1540
  833.4 7.4 copy-start.24
Sparse Core Ops, SparseCore 0:
  10.0 83.3 all-gather.1
  111.4 69.4 all-reduce.32
  199.8 70.3 all-reduce.30
  289.0 70.3 all-reduce.28
  378.3 70.3 all-reduce.26
  467.5 70.4 all-reduce.24
  556.8 70.3 all-reduce.22
  646.1 70.3 all-reduce.20
  735.4 70.3 all-reduce.18
where the time goes:
time: 849 us; the launch traced here: 847 us
  waiting for transfers between devices  637 us (75%)
  matrix products  144 us (17%)
  blocking collectives  26.2 us (3%)
  other arithmetic  19 us (2%)
  between operations  15.8 us (2%)
    psum x8, waiting for transfers between devices, rollout(): change = lax.psum(partial_change, 'tp')  559 us
    dot_general x32, matrix products, rollout(): jnp.einsum('mck,mkh->mch', hidden_one, hid_rows, preferred_element_type=j...  118 us
    all_gather x1, waiting for transfers between devices, on_device(): input_layer = lax.all_gather(w_in, 'tp', axis=2, tiled=True)  77.4 us
    dot_general x32, matrix products, rollout(): jnp.einsum('mck,mks->mcs', hidden_two, out_rows, preferred_element_type=j...  24.4 us
  transfers between devices with their start and end apart: 9, of which 9 were waited for; matrix products, arithmetic and copies ran while one was open for 1% of the time, Pallas kernels for 0%

commit v1 on v0

--- a/solution.py
+++ b/solution.py
@@ -4,6 +4,17 @@
 from jax.sharding import PartitionSpec as P
 
 HORIZON = 8
+
+
+def gather_by_hops(x, mesh_axis, along):
+    count = lax.axis_size(mesh_axis)
+    forward = [(i, (i + 1) % count) for i in range(count)]
+    terms = [x]
+    for far in range(1, count):
+        terms = [lax.ppermute(terms[0], mesh_axis, forward), *terms]
+    whole = jnp.concatenate(terms, axis=along)
+    shift = (lax.axis_index(mesh_axis) + 1) * terms[-1].shape[along]
+    return jnp.roll(whole, shift, axis=along)
 
 
 def reward_of(states, goal, action):
@@ -26,7 +37,7 @@
     ).astype(jnp.float32)
     slot_actions = jnp.dot(dispatch, actions, precision=lax.Precision.HIGHEST)
     slot_actions = slot_actions.reshape(member_count, capacity, HORIZON, action_width)
-    input_layer = lax.all_gather(w_in, "tp", axis=2, tiled=True)
+    input_layer = gather_by_hops(w_in, "tp", 2)
 
     def rollout(first, count):
         layer_in = input_layer[first : first + count]

time: 849 us -> 897 us (1.057)
  local copies, waits for them, and re-layouts: 3.87 us -> 28.7 us
  waiting for transfers between devices: 637 us -> 647 us
  other arithmetic: 19 us -> 28.3 us
    ppermute x0 -> x7, waiting for transfers between devices: none -> 86.8 us  [gather_by_hops(): terms = [lax.ppermute(terms[0], mesh_axis, forward), *terms]]
    all_gather x1 -> x0, waiting for transfers between devices: 77.4 us -> none  [on_device(): input_layer = lax.all_gather(w_in, 'tp', axis=2, tiled=True)]
    unnamed x81 -> x172, local copies, waits for them, and re-layouts: 2.76 us -> 23.1 us
    reduce_sum x20, other arithmetic: 2.29 us -> 11.5 us  [reward_of(): jnp.mean(action * action, axis=-1)]
  transfers between devices with their start and end apart: 9 -> 15, of which waited for: 9 -> 15; matrix products, arithmetic and copies ran while one was open for 1% -> 3% of each run, Pallas kernels for 0% -> 0%
where the time goes in v1:
time: 897 us; the launch traced here: 895 us
  waiting for transfers between devices  647 us (72%)
  matrix products  145 us (16%)
  local copies, waits for them, and re-layouts  28.7 us (3%)
  other arithmetic  28.3 us (3%)
  blocking collectives  26.2 us (3%)
  between operations  16.4 us (2%)
    psum x8, waiting for transfers between devices, rollout(): change = lax.psum(partial_change, 'tp')  560 us
    dot_general x32, matrix products, rollout(): jnp.einsum('mck,mkh->mch', hidden_one, hid_rows, preferred_element_type=j...  119 us
    ppermute x7, waiting for transfers between devices, gather_by_hops(): terms = [lax.ppermute(terms[0], mesh_axis, forward), *terms]  86.8 us
    dot_general x32, matrix products, rollout(): jnp.einsum('mck,mks->mcs', hidden_two, out_rows, preferred_element_type=j...  24.4 us
    unnamed x172, local copies, waits for them, and re-layouts  23.1 us
  transfers between devices with their start and end apart: 15, of which 15 were waited for; matrix products, arithmetic and copies ran while one was open for 3% of the time, Pallas kernels for 0%

profile of v1, /device:TPU:0, one launch (start us, length us, event | category | flops | bytes accessed | tf_op | source)
XLA Modules:
  0.0 895.4 jit_solution(8284034405872690123)
XLA Ops:
  7.2 3.0 collective-permute-start
  10.3 16.6 %collective-permute-done = bf16[4,144,512]{2,1,0:T(8,128)(2,1)S(1)} collective-permute-done((bf16[4,144,512]{2,1,0:T(8,128)(2,1)}, bf16[4,144,512]{2,1,0:T(8,128)(2,1)S(1)}, u32[]{:S(2)}, u32[]{:S(2)}) %collective-permute-start) | collective-permute-done | bytes 589856 | tf_op jit(solution)/shard_map/ppermute | solution.py:14
  26.8 17.2 %collective-permute-done.1 = bf16[4,144,512]{2,1,0:T(8,128)(2,1)S(1)} collective-permute-done((bf16[4,144,512]{2,1,0:T(8,128)(2,1)S(1)}, bf16[4,144,512]{2,1,0:T(8,128)(2,1)S(1)}, u32[]{:S(2)}, u32[]{:S(2)}) %collective-permute-start.1) | collective-permute-done | bytes 589856 | tf_op jit(solution)/shard_map/ppermute | solution.py:14
  44.0 16.3 %collective-permute-done.2 = bf16[4,144,512]{2,1,0:T(8,128)(2,1)S(1)} collective-permute-done((bf16[4,144,512]{2,1,0:T(8,128)(2,1)S(1)}, bf16[4,144,512]{2,1,0:T(8,128)(2,1)S(1)}, u32[]{:S(2)}, u32[]{:S(2)}) %collective-permute-start.2) | collective-permute-done | bytes 589856 | tf_op jit(solution)/shard_map/ppermute | solution.py:14
  62.6 13.2 %collective-permute-done.3 = bf16[4,144,512]{2,1,0:T(8,128)(2,1)S(1)} collective-permute-done((bf16[4,144,512]{2,1,0:T(8,128)(2,1)S(1)}, bf16[4,144,512]{2,1,0:T(8,128)(2,1)S(1)}, u32[]{:S(2)}, u32[]{:S(2)}) %collective-permute-start.3) | collective-permute-done | bytes 589856 | tf_op jit(solution)/shard_map/ppermute | solution.py:14
  78.7 11.9 %collective-permute-done.4 = bf16[4,144,512]{2,1,0:T(8,128)(2,1)} collective-permute-done((bf16[4,144,512]{2,1,0:T(8,128)(2,1)S(1)}, bf16[4,144,512]{2,1,0:T(8,128)(2,1)}, u32[]{:S(2)}, u32[]{:S(2)}) %collective-permute-start.4) | collective-permute-done | bytes 589856 | tf_op jit(solution)/shard_map/ppermute | solution.py:14
  91.4 1.3 multiply_reduce_fusion.63
  94.0 10.6 %collective-permute-done.5 = bf16[4,144,512]{2,1,0:T(8,128)(2,1)} collective-permute-done((bf16[4,144,512]{2,1,0:T(8,128)(2,1)}, bf16[4,144,512]{2,1,0:T(8,128)(2,1)}, u32[]{:S(2)}, u32[]{:S(2)}) %collective-permute-start.5) | collective-permute-done | bytes 589856 | tf_op jit(solution)/shard_map/ppermute | solution.py:14
  104.7 1.3 multiply_reduce_fusion.12
  110.5 1.3 multiply_reduce_fusion.27
  113.0 1.3 multiply_reduce_fusion.55
  114.3 1.3 multiply_reduce_fusion.10
  115.6 1.3 multiply_reduce_fusion.25
  117.9 2.0 constant_dynamic-update-slice_fusion.15
  119.9 2.0 constant_dynamic-update-slice_fusion.14
  121.9 2.0 constant_dynamic-update-slice_fusion.13
  128.5 2.0 constant_dynamic-update-slice_fusion.7
  130.5 2.0 constant_dynamic-update-slice_fusion.6
  132.5 2.0 constant_dynamic-update-slice_fusion.5
  139.1 3.7 multiply_convert_fusion.157
  143.6 3.7 multiply_convert_fusion.85
  148.1 3.7 multiply_convert_fusion.109
  152.6 3.7 multiply_convert_fusion.133
  157.6 70.5 %all-reduce.33.cloned.1.call-done = (f32[1,60,128]{2,1,0:T(8,128)}, f32[1,60,128]{2,1,0:T(8,128)}, f32[1,60,128]{2,1,0:T(8,128)}, f32[1,60,128]{2,1,0:T(8,128)}) async-done(((f32[1,60,128]{2,1,0:T(8,128)}, f32[1,60,128]{2,1,0:T(8,128)}, f32[1,60,128]{2,1,0:T(8,128)}, f32[1,60,128]{2,1,0:T(8,128)}), (f32[1,60,128]{2,1,0:T(8,128)}, f32[1,60,128]{2,1,0:T(8,128)}, f32[1,60,128]{2,1,0:T(8,128)}, ...) | async-done | bytes 122896 | tf_op jit(solution)/shard_map/psum | solution.py:62
  228.9 3.7 multiply_convert_fusion.154
  233.4 3.7 multiply_convert_fusion.82
  238.0 3.7 multiply_convert_fusion.106
  242.5 3.7 multiply_convert_fusion.130
  247.7 69.8 %all-reduce.31.cloned.1.call-done = (f32[1,60,128]{2,1,0:T(8,128)}, f32[1,60,128]{2,1,0:T(8,128)}, f32[1,60,128]{2,1,0:T(8,128)}, f32[1,60,128]{2,1,0:T(8,128)}) async-done(((f32[1,60,128]{2,1,0:T(8,128)}, f32[1,60,128]{2,1,0:T(8,128)}, f32[1,60,128]{2,1,0:T(8,128)}, f32[1,60,128]{2,1,0:T(8,128)}), (f32[1,60,128]{2,1,0:T(8,128)}, f32[1,60,128]{2,1,0:T(8,128)}, f32[1,60,128]{2,1,0:T(8,128)}, ...) | async-done | bytes 122896 | tf_op jit(solution)/shard_map/psum | solution.py:62
  318.3 3.7 multiply_convert_fusion.151
  322.8 3.7 multiply_convert_fusion.79
  327.3 3.7 multiply_convert_fusion.103
  331.8 3.7 multiply_convert_fusion.127
  336.9 69.9 %all-reduce.29.cloned.1.call-done = (f32[1,60,128]{2,1,0:T(8,128)}, f32[1,60,128]{2,1,0:T(8,128)}, f32[1,60,128]{2,1,0:T(8,128)}, f32[1,60,128]{2,1,0:T(8,128)}) async-done(((f32[1,60,128]{2,1,0:T(8,128)}, f32[1,60,128]{2,1,0:T(8,128)}, f32[1,60,128]{2,1,0:T(8,128)}, f32[1,60,128]{2,1,0:T(8,128)}), (f32[1,60,128]{2,1,0:T(8,128)}, f32[1,60,128]{2,1,0:T(8,128)}, f32[1,60,128]{2,1,0:T(8,128)}, ...) | async-done | bytes 122896 | tf_op jit(solution)/shard_map/psum | solution.py:62
  407.6 3.7 multiply_convert_fusion.148
  412.1 3.7 multiply_convert_fusion.76
  416.6 3.7 multiply_convert_fusion.100
  421.1 3.7 multiply_convert_fusion.124
  426.2 69.9 %all-reduce.27.cloned.1.call-done = (f32[1,60,128]{2,1,0:T(8,128)}, f32[1,60,128]{2,1,0:T(8,128)}, f32[1,60,128]{2,1,0:T(8,128)}, f32[1,60,128]{2,1,0:T(8,128)}) async-done(((f32[1,60,128]{2,1,0:T(8,128)}, f32[1,60,128]{2,1,0:T(8,128)}, f32[1,60,128]{2,1,0:T(8,128)}, f32[1,60,128]{2,1,0:T(8,128)}), (f32[1,60,128]{2,1,0:T(8,128)}, f32[1,60,128]{2,1,0:T(8,128)}, f32[1,60,128]{2,1,0:T(8,128)}, ...) | async-done | bytes 122896 | tf_op jit(solution)/shard_map/psum | solution.py:62
  496.8 3.7 multiply_convert_fusion.145
  501.3 3.7 multiply_convert_fusion.73
  505.8 3.7 multiply_convert_fusion.97
  510.3 3.7 multiply_convert_fusion.121
  515.7 69.7 %all-reduce.25.cloned.1.call-done = (f32[1,60,128]{2,1,0:T(8,128)}, f32[1,60,128]{2,1,0:T(8,128)}, f32[1,60,128]{2,1,0:T(8,128)}, f32[1,60,128]{2,1,0:T(8,128)}) async-done(((f32[1,60,128]{2,1,0:T(8,128)}, f32[1,60,128]{2,1,0:T(8,128)}, f32[1,60,128]{2,1,0:T(8,128)}, f32[1,60,128]{2,1,0:T(8,128)}), (f32[1,60,128]{2,1,0:T(8,128)}, f32[1,60,128]{2,1,0:T(8,128)}, f32[1,60,128]{2,1,0:T(8,128)}, ...) | async-done | bytes 122896 | tf_op jit(solution)/shard_map/psum | solution.py:62
  586.1 3.7 multiply_convert_fusion.142
  590.6 3.7 multiply_convert_fusion.70
  595.1 3.7 multiply_convert_fusion.94
  599.6 3.7 multiply_convert_fusion.118
  604.7 70.0 %all-reduce.23.cloned.1.call-done = (f32[1,60,128]{2,1,0:T(8,128)}, f32[1,60,128]{2,1,0:T(8,128)}, f32[1,60,128]{2,1,0:T(8,128)}, f32[1,60,128]{2,1,0:T(8,128)}) async-done(((f32[1,60,128]{2,1,0:T(8,128)}, f32[1,60,128]{2,1,0:T(8,128)}, f32[1,60,128]{2,1,0:T(8,128)}, f32[1,60,128]{2,1,0:T(8,128)}), (f32[1,60,128]{2,1,0:T(8,128)}, f32[1,60,128]{2,1,0:T(8,128)}, f32[1,60,128]{2,1,0:T(8,128)}, ...) | async-done | bytes 122896 | tf_op jit(solution)/shard_map/psum | solution.py:62
  675.4 3.7 multiply_convert_fusion.139
  679.9 3.7 multiply_convert_fusion.67
  684.4 3.7 multiply_convert_fusion.91
  688.9 3.7 multiply_convert_fusion.115
  693.8 70.1 %all-reduce.21.cloned.1.call-done = (f32[1,60,128]{2,1,0:T(8,128)}, f32[1,60,128]{2,1,0:T(8,128)}, f32[1,60,128]{2,1,0:T(8,128)}, f32[1,60,128]{2,1,0:T(8,128)}) async-done(((f32[1,60,128]{2,1,0:T(8,128)}, f32[1,60,128]{2,1,0:T(8,128)}, f32[1,60,128]{2,1,0:T(8,128)}, f32[1,60,128]{2,1,0:T(8,128)}), (f32[1,60,128]{2,1,0:T(8,128)}, f32[1,60,128]{2,1,0:T(8,128)}, f32[1,60,128]{2,1,0:T(8,128)}, ...) | async-done | bytes 122896 | tf_op jit(solution)/shard_map/psum | solution.py:62
  764.7 3.7 multiply_convert_fusion.136
  769.2 3.7 multiply_convert_fusion.64
  773.8 3.7 multiply_convert_fusion.88
  778.4 3.7 multiply_convert_fusion.112
  782.9 70.5 %all-reduce.19.cloned.1.call-done = (f32[1,60,128]{2,1,0:T(8,128)}, f32[1,60,128]{2,1,0:T(8,128)}, f32[1,60,128]{2,1,0:T(8,128)}, f32[1,60,128]{2,1,0:T(8,128)}) async-done(((f32[1,60,128]{2,1,0:T(8,128)}, f32[1,60,128]{2,1,0:T(8,128)}, f32[1,60,128]{2,1,0:T(8,128)}, f32[1,60,128]{2,1,0:T(8,128)}), (f32[1,60,128]{2,1,0:T(8,128)}, f32[1,60,128]{2,1,0:T(8,128)}, f32[1,60,128]{2,1,0:T(8,128)}, ...) | async-done | bytes 122896 | tf_op jit(solution)/shard_map/psum | solution.py:62
  854.6 1.2 multiply_reduce_fusion.33
  856.9 6.3 psum.291
  864.5 7.2 psum.292
  873.8 6.6 all-reduce.9
  881.3 6.0 psum.295
  (296 shorter events, 64.2 us)
Async XLA Ops:
  7.2 120.5 %copy-start.1 = (bf16[4,144,512]{2,1,0:T(8,128)(2,1)S(1)}, bf16[4,144,512]{2,1,0:T(8,128)(2,1)}, u32[]{:S(2)}) copy-start(bf16[4,144,512]{2,1,0:T(8,128)(2,1)} %param.17) | copy-start | bytes 1769476
  7.2 220.9 %all-reduce.33.cloned.1.call-start = ((), (), s32[]{:S(2)}) async-start(), calls=%async_computation.7 | async-start | bytes 262144 | tf_op jit(solution)/shard_map/psum | solution.py:62
  7.2 19.6 %collective-permute-start = (bf16[4,144,512]{2,1,0:T(8,128)(2,1)}, bf16[4,144,512]{2,1,0:T(8,128)(2,1)S(1)}, u32[]{:S(2)}, u32[]{:S(2)}) collective-permute-start(bf16[4,144,512]{2,1,0:T(8,128)(2,1)} %param.17), channel_id=1, source_target_pairs={{0,1},{1,2},{2,3},{3,4},{4,5},{5,6},{6,7},{7,0},{8,9},{9,10},{10,1... | collective-permute-start | bytes 1769480 | tf_op jit(solution)/shard_map/ppermute | solution.py:14
  26.8 17.2 %collective-permute-start.1 = (bf16[4,144,512]{2,1,0:T(8,128)(2,1)S(1)}, bf16[4,144,512]{2,1,0:T(8,128)(2,1)S(1)}, u32[]{:S(2)}, u32[]{:S(2)}) collective-permute-start(bf16[4,144,512]{2,1,0:T(8,128)(2,1)S(1)} %collective-permute-done), channel_id=1, source_target_pairs={{0,1},{1,2},{2,3},{3,4},{4,5},{5,6},{6,7},{7,0},{8,9},{9,10},{10,1... | collective-permute-start | bytes 1769480 | tf_op jit(solution)/shard_map/ppermute | solution.py:14
  44.0 16.3 %collective-permute-start.2 = (bf16[4,144,512]{2,1,0:T(8,128)(2,1)S(1)}, bf16[4,144,512]{2,1,0:T(8,128)(2,1)S(1)}, u32[]{:S(2)}, u32[]{:S(2)}) collective-permute-start(bf16[4,144,512]{2,1,0:T(8,128)(2,1)S(1)} %collective-permute-done.1), channel_id=1, source_target_pairs={{0,1},{1,2},{2,3},{3,4},{4,5},{5,6},{6,7},{7,0},{8,9},{9,10},{10,1... | collective-permute-start | bytes 1769480 | tf_op jit(solution)/shard_map/ppermute | solution.py:14
  60.4 15.5 %collective-permute-start.3 = (bf16[4,144,512]{2,1,0:T(8,128)(2,1)S(1)}, bf16[4,144,512]{2,1,0:T(8,128)(2,1)S(1)}, u32[]{:S(2)}, u32[]{:S(2)}) collective-permute-start(bf16[4,144,512]{2,1,0:T(8,128)(2,1)S(1)} %collective-permute-done.2), channel_id=1, source_target_pairs={{0,1},{1,2},{2,3},{3,4},{4,5},{5,6},{6,7},{7,0},{8,9},{9,10},{10,1... | collective-permute-start | bytes 1769480 | tf_op jit(solution)/shard_map/ppermute | solution.py:14
  75.8 14.7 %collective-permute-start.4 = (bf16[4,144,512]{2,1,0:T(8,128)(2,1)S(1)}, bf16[4,144,512]{2,1,0:T(8,128)(2,1)}, u32[]{:S(2)}, u32[]{:S(2)}) collective-permute-start(bf16[4,144,512]{2,1,0:T(8,128)(2,1)S(1)} %collective-permute-done.3), channel_id=1, source_target_pairs={{0,1},{1,2},{2,3},{3,4},{4,5},{5,6},{6,7},{7,0},{8,9},{9,10},{10,1... | collective-permute-start | bytes 1769480 | tf_op jit(solution)/shard_map/ppermute | solution.py:14
  77.3 51.2 %copy-start.47 = (s32[192]{0:T(256)}, s32[192]{0:T(256)S(1)}, u32[]{:S(2)}) copy-start(s32[192]{0:T(256)S(1)} %convert_add_fusion) | copy-start | bytes 2308
  90.6 14.1 %collective-permute-start.5 = (bf16[4,144,512]{2,1,0:T(8,128)(2,1)}, bf16[4,144,512]{2,1,0:T(8,128)(2,1)}, u32[]{:S(2)}, u32[]{:S(2)}) collective-permute-start(bf16[4,144,512]{2,1,0:T(8,128)(2,1)} %collective-permute-done.4), channel_id=1, source_target_pairs={{0,1},{1,2},{2,3},{3,4},{4,5},{5,6},{6,7},{7,0},{8,9},{9,10},{10,1... | collective-permute-start | bytes 1769480 | tf_op jit(solution)/shard_map/ppermute | solution.py:14
  104.7 13.2 %collective-permute-start.6 = (bf16[4,144,512]{2,1,0:T(8,128)(2,1)}, bf16[4,144,512]{2,1,0:T(8,128)(2,1)}, u32[]{:S(2)}, u32[]{:S(2)}) collective-permute-start(bf16[4,144,512]{2,1,0:T(8,128)(2,1)} %collective-permute-done.5), channel_id=1, source_target_pairs={{0,1},{1,2},{2,3},{3,4},{4,5},{5,6},{6,7},{7,0},{8,9},{9,10},{10,1... | collective-permute-start | bytes 1769480 | tf_op jit(solution)/shard_map/ppermute | solution.py:14
  130.5 12.3 %copy-start = (bf16[4,512,128]{2,1,0:T(8,128)(2,1)S(1)}, bf16[4,512,128]{2,1,0:T(8,128)(2,1)}, u32[]{:S(2)}) copy-start(bf16[4,512,128]{2,1,0:T(8,128)(2,1)} %param.19) | copy-start | bytes 1572868
  139.1 9.0 %copy-start.42 = (bf16[1,60,1,16]{3,1,2,0:T(8,128)(2,1)S(1)}, bf16[1,60,1,16]{3,1,2,0:T(8,128)(2,1)}, u32[]{:S(2)}) copy-start(bf16[1,60,1,16]{3,1,2,0:T(8,128)(2,1)} %copy.116) | copy-start | bytes 5764
  139.1 9.0 %copy-start.63 = (bf16[144]{0:T(256)(128)(2,1)S(1)}, bf16[144]{0:T(256)(128)(2,1)}, u32[]{:S(2)}) copy-start(bf16[144]{0:T(256)(128)(2,1)} %pad.71.clone) | copy-start | bytes 868
  143.6 9.0 %copy-start.43 = (bf16[1,60,1,16]{3,1,2,0:T(8,128)(2,1)S(1)}, bf16[1,60,1,16]{3,1,2,0:T(8,128)(2,1)}, u32[]{:S(2)}) copy-start(bf16[1,60,1,16]{3,1,2,0:T(8,128)(2,1)} %copy.115) | copy-start | bytes 5764
  148.1 9.2 %copy-start.34 = (f32[1,60,1,16]{1,0,3,2:T(1,128)S(1)}, f32[1,60,1,16]{1,0,3,2:T(1,128)}, u32[]{:S(2)}) copy-start(f32[1,60,1,16]{1,0,3,2:T(1,128)} %get-tuple-element.154) | copy-start | bytes 11524
  148.1 9.3 %copy-start.25 = (f32[1,60,1,16]{1,0,3,2:T(1,128)S(1)}, f32[1,60,1,16]{1,0,3,2:T(1,128)}, u32[]{:S(2)}) copy-start(f32[1,60,1,16]{1,0,3,2:T(1,128)} %get-tuple-element.140) | copy-start | bytes 11524
  148.1 80.0 %copy-start.46 = (f32[128]{0:T(128)S(1)}, f32[128]{0:T(128)}, u32[]{:S(2)}) copy-start(f32[128]{0:T(128)} %param.10) | copy-start | bytes 1540
  148.1 80.8 %copy-start.35 = (bf16[60,16]{1,0:T(8,128)(2,1)S(1)}, bf16[60,16]{1,0:T(8,128)(2,1)}, u32[]{:S(2)}) copy-start(bf16[60,16]{1,0:T(8,128)(2,1)} %get-tuple-element.163) | copy-start | bytes 5764
  152.6 80.8 %copy-start.36 = (bf16[60,16]{1,0:T(8,128)(2,1)S(1)}, bf16[60,16]{1,0:T(8,128)(2,1)}, u32[]{:S(2)}) copy-start(bf16[60,16]{1,0:T(8,128)(2,1)} %get-tuple-element.205) | copy-start | bytes 5764
  157.1 160.3 %all-reduce.31.cloned.1.call-start = ((), (), s32[]{:S(2)}) async-start(), calls=%async_computation.6 | async-start | bytes 262144 | tf_op jit(solution)/shard_map/psum | solution.py:62
  233.4 9.1 %copy-start.40 = (bf16[60,16]{1,0:T(8,128)(2,1)S(1)}, bf16[60,16]{1,0:T(8,128)(2,1)}, u32[]{:S(2)}) copy-start(bf16[60,16]{1,0:T(8,128)(2,1)} %get-tuple-element.177) | copy-start | bytes 5764
  237.9 9.4 %copy-start.24 = (f32[1,60,1,16]{1,0,3,2:T(1,128)S(1)}, f32[1,60,1,16]{1,0,3,2:T(1,128)}, u32[]{:S(2)}) copy-start(f32[1,60,1,16]{1,0,3,2:T(1,128)} %get-tuple-element.133) | copy-start | bytes 11524
  237.9 9.5 %copy-start.23 = (f32[1,60,1,16]{1,0,3,2:T(1,128)S(1)}, f32[1,60,1,16]{1,0,3,2:T(1,128)}, u32[]{:S(2)}) copy-start(f32[1,60,1,16]{1,0,3,2:T(1,128)} %get-tuple-element.132) | copy-start | bytes 11524
  237.9 9.6 %copy-start.33 = (f32[1,60,1,16]{1,0,3,2:T(1,128)S(1)}, f32[1,60,1,16]{1,0,3,2:T(1,128)}, u32[]{:S(2)}) copy-start(f32[1,60,1,16]{1,0,3,2:T(1,128)} %get-tuple-element.148) | copy-start | bytes 11524
  237.9 79.6 %copy-start.3 = (f32[1,60,128]{2,1,0:T(8,128)S(1)}, f32[1,60,128]{2,1,0:T(8,128)}, u32[]{:S(2)}) copy-start(f32[1,60,128]{2,1,0:T(8,128)} %get-tuple-element.73) | copy-start | bytes 92164
  237.9 79.6 %copy-start.4 = (f32[1,60,128]{2,1,0:T(8,128)S(1)}, f32[1,60,128]{2,1,0:T(8,128)}, u32[]{:S(2)}) copy-start(f32[1,60,128]{2,1,0:T(8,128)} %get-tuple-element.74) | copy-start | bytes 92164
  237.9 79.5 %copy-start.5 = (f32[1,60,128]{2,1,0:T(8,128)S(1)}, f32[1,60,128]{2,1,0:T(8,128)}, u32[]{:S(2)}) copy-start(f32[1,60,128]{2,1,0:T(8,128)} %get-tuple-element.75) | copy-start | bytes 92164
  237.9 79.5 %copy-start.6 = (f32[1,60,128]{2,1,0:T(8,128)S(1)}, f32[1,60,128]{2,1,0:T(8,128)}, u32[]{:S(2)}) copy-start(f32[1,60,128]{2,1,0:T(8,128)} %get-tuple-element.76) | copy-start | bytes 92164
  238.0 80.4 %copy-start.39 = (bf16[60,16]{1,0:T(8,128)(2,1)S(1)}, bf16[60,16]{1,0:T(8,128)(2,1)}, u32[]{:S(2)}) copy-start(bf16[60,16]{1,0:T(8,128)(2,1)} %get-tuple-element.165) | copy-start | bytes 5764
  242.5 80.3 %copy-start.38 = (bf16[60,16]{1,0:T(8,128)(2,1)S(1)}, bf16[60,16]{1,0:T(8,128)(2,1)}, u32[]{:S(2)}) copy-start(bf16[60,16]{1,0:T(8,128)(2,1)} %get-tuple-element.207) | copy-start | bytes 5764
  247.0 159.8 %all-reduce.29.cloned.1.call-start = ((), (), s32[]{:S(2)}) async-start(), calls=%async_computation.5 | async-start | bytes 262144 | tf_op jit(solution)/shard_map/psum | solution.py:62
  327.3 9.2 %copy-start.32 = (f32[1,60,1,16]{1,0,3,2:T(1,128)S(1)}, f32[1,60,1,16]{1,0,3,2:T(1,128)}, u32[]{:S(2)}) copy-start(f32[1,60,1,16]{1,0,3,2:T(1,128)} %get-tuple-element.153) | copy-start | bytes 11524
  327.3 9.3 %copy-start.31 = (f32[1,60,1,16]{1,0,3,2:T(1,128)S(1)}, f32[1,60,1,16]{1,0,3,2:T(1,128)}, u32[]{:S(2)}) copy-start(f32[1,60,1,16]{1,0,3,2:T(1,128)} %get-tuple-element.152) | copy-start | bytes 11524
  327.3 9.3 %copy-start.22 = (f32[1,60,1,16]{1,0,3,2:T(1,128)S(1)}, f32[1,60,1,16]{1,0,3,2:T(1,128)}, u32[]{:S(2)}) copy-start(f32[1,60,1,16]{1,0,3,2:T(1,128)} %get-tuple-element.139) | copy-start | bytes 11524
  327.3 9.4 %copy-start.21 = (f32[1,60,1,16]{1,0,3,2:T(1,128)S(1)}, f32[1,60,1,16]{1,0,3,2:T(1,128)}, u32[]{:S(2)}) copy-start(f32[1,60,1,16]{1,0,3,2:T(1,128)} %get-tuple-element.138) | copy-start | bytes 11524
  336.3 159.8 %all-reduce.27.cloned.1.call-start = ((), (), s32[]{:S(2)}) async-start(), calls=%async_computation.4 | async-start | bytes 262144 | tf_op jit(solution)/shard_map/psum | solution.py:62
  416.6 9.1 %copy-start.30 = (f32[1,60,1,16]{1,0,3,2:T(1,128)S(1)}, f32[1,60,1,16]{1,0,3,2:T(1,128)}, u32[]{:S(2)}) copy-start(f32[1,60,1,16]{1,0,3,2:T(1,128)} %get-tuple-element.147) | copy-start | bytes 11524
  416.6 9.2 %copy-start.29 = (f32[1,60,1,16]{1,0,3,2:T(1,128)S(1)}, f32[1,60,1,16]{1,0,3,2:T(1,128)}, u32[]{:S(2)}) copy-start(f32[1,60,1,16]{1,0,3,2:T(1,128)} %get-tuple-element.146) | copy-start | bytes 11524
  425.5 159.8 %all-reduce.25.cloned.1.call-start = ((), (), s32[]{:S(2)}) async-start(), calls=%async_computation.3 | async-start | bytes 262144 | tf_op jit(solution)/shard_map/psum | solution.py:62
  501.3 9.0 %copy-start.9 = (f32[1,60,128]{2,1,0:T(8,128)S(1)}, f32[1,60,128]{2,1,0:T(8,128)}, u32[]{:S(2)}) copy-start(f32[1,60,128]{2,1,0:T(8,128)} %get-tuple-element.61) | copy-start | bytes 92164
  505.8 9.4 %copy-start.28 = (f32[1,60,1,16]{1,0,3,2:T(1,128)S(1)}, f32[1,60,1,16]{1,0,3,2:T(1,128)}, u32[]{:S(2)}) copy-start(f32[1,60,1,16]{1,0,3,2:T(1,128)} %get-tuple-element.151) | copy-start | bytes 11524
  505.8 9.5 %copy-start.27 = (f32[1,60,1,16]{1,0,3,2:T(1,128)S(1)}, f32[1,60,1,16]{1,0,3,2:T(1,128)}, u32[]{:S(2)}) copy-start(f32[1,60,1,16]{1,0,3,2:T(1,128)} %get-tuple-element.145) | copy-start | bytes 11524
  514.8 159.8 %all-reduce.23.cloned.1.call-start = ((), (), s32[]{:S(2)}) async-start(), calls=%async_computation.2 | async-start | bytes 262144 | tf_op jit(solution)/shard_map/psum | solution.py:62
  595.1 9.3 %copy-start.26 = (f32[1,60,1,16]{1,0,3,2:T(1,128)S(1)}, f32[1,60,1,16]{1,0,3,2:T(1,128)}, u32[]{:S(2)}) copy-start(f32[1,60,1,16]{1,0,3,2:T(1,128)} %get-tuple-element.157) | copy-start | bytes 11524
  604.1 159.8 %all-reduce.21.cloned.1.call-start = ((), (), s32[]{:S(2)}) async-start(), calls=%async_computation.1 | async-start | bytes 262144 | tf_op jit(solution)/shard_map/psum | solution.py:62
  693.4 160.0 %all-reduce.19.cloned.1.call-start = ((), (), s32[]{:S(2)}) async-start(), calls=%async_computation | async-start | bytes 262144 | tf_op jit(solution)/shard_map/psum | solution.py:62
  769.2 9.2 %copy-start.13 = (f32[1,60,128]{2,1,0:T(8,128)S(1)}, f32[1,60,128]{2,1,0:T(8,128)}, u32[]{:S(2)}) copy-start(f32[1,60,128]{2,1,0:T(8,128)} %get-tuple-element.49) | copy-start | bytes 92164
  773.7 79.7 %copy-start.60 = (f32[128]{0:T(128)S(1)}, f32[128]{0:T(128)}, u32[]{:S(2)}) copy-start(f32[128]{0:T(128)} %param.11) | copy-start | bytes 1540
  773.7 82.1 %copy-start.53 = (f32[60]{0:T(128)S(1)}, f32[60]{0:T(128)}, u32[]{:S(2)}) copy-start(f32[60]{0:T(128)} %get-tuple-element.3) | copy-start | bytes 724
  773.7 82.1 %copy-start.54 = (f32[60]{0:T(128)S(1)}, f32[60]{0:T(128)}, u32[]{:S(2)}) copy-start(f32[60]{0:T(128)} %get-tuple-element.162) | copy-start | bytes 724
  773.7 82.1 %copy-start.59 = (f32[60]{0:T(128)S(1)}, f32[60]{0:T(128)}, u32[]{:S(2)}) copy-start(f32[60]{0:T(128)} %get-tuple-element.164) | copy-start | bytes 724
  773.7 82.1 %copy-start.52 = (f32[60]{0:T(128)S(1)}, f32[60]{0:T(128)}, u32[]{:S(2)}) copy-start(f32[60]{0:T(128)} %get-tuple-element.4) | copy-start | bytes 724
  773.7 82.1 %copy-start.58 = (f32[60]{0:T(128)S(1)}, f32[60]{0:T(128)}, u32[]{:S(2)}) copy-start(f32[60]{0:T(128)} %get-tuple-element.176) | copy-start | bytes 724
  773.7 82.2 %copy-start.51 = (f32[60]{0:T(128)S(1)}, f32[60]{0:T(128)}, u32[]{:S(2)}) copy-start(f32[60]{0:T(128)} %get-tuple-element.5) | copy-start | bytes 724
  773.7 82.2 %copy-start.56 = (f32[60]{0:T(128)S(1)}, f32[60]{0:T(128)}, u32[]{:S(2)}) copy-start(f32[60]{0:T(128)} %get-tuple-element.190) | copy-start | bytes 724
  773.7 82.2 %copy-start.57 = (f32[60]{0:T(128)S(1)}, f32[60]{0:T(128)}, u32[]{:S(2)}) copy-start(f32[60]{0:T(128)} %get-tuple-element.192) | copy-start | bytes 724
  773.8 82.2 %copy-start.49 = (f32[60]{0:T(128)S(1)}, f32[60]{0:T(128)}, u32[]{:S(2)}) copy-start(f32[60]{0:T(128)} %get-tuple-element.6) | copy-start | bytes 724
  773.8 82.2 %copy-start.50 = (f32[60]{0:T(128)S(1)}, f32[60]{0:T(128)}, u32[]{:S(2)}) copy-start(f32[60]{0:T(128)} %get-tuple-element.204) | copy-start | bytes 724
  773.8 82.2 %copy-start.55 = (f32[60]{0:T(128)S(1)}, f32[60]{0:T(128)}, u32[]{:S(2)}) copy-start(f32[60]{0:T(128)} %get-tuple-element.206) | copy-start | bytes 724
  773.8 82.3 %copy-start.48 = (s32[192]{0:T(256)S(1)}, s32[192]{0:T(256)}, u32[]{:S(2)}) copy-start(s32[192]{0:T(256)} %copy-done.47) | copy-start | bytes 2308
  773.8 90.6 %copy-start.62 = (s32[96]{0:T(128)S(1)}, s32[96]{0:T(128)}, u32[]{:S(2)}) copy-start(s32[96]{0:T(128)} %param.16) | copy-start | bytes 1156
  773.8 99.8 %copy-start.2 = (f32[192,128]{1,0:T(8,128)S(1)}, f32[192,128]{1,0:T(8,128)}, u32[]{:S(2)}) copy-start(f32[192,128]{1,0:T(8,128)} %param.14) | copy-start | bytes 294916
  773.8 99.8 %copy-start.44 = (f32[128]{0:T(128)S(1)}, f32[128]{0:T(128)}, u32[]{:S(2)}) copy-start(f32[128]{0:T(128)} %param.13) | copy-start | bytes 1540
  773.8 99.8 %copy-start.45 = (f32[128]{0:T(128)S(1)}, f32[128]{0:T(128)}, u32[]{:S(2)}) copy-start(f32[128]{0:T(128)} %param.12) | copy-start | bytes 1540
  (15 other events, 110.7 us)
Sparse Core Ops, SparseCore 0:
  157.2 70.8 all-reduce.32
  247.1 70.3 all-reduce.30
  336.4 70.3 all-reduce.28
  425.7 70.3 all-reduce.26
  514.9 70.3 all-reduce.24
  604.2 70.3 all-reduce.22
  693.5 70.3 all-reduce.20
  783.0 70.3 all-reduce.18
